TPU v7x, 256 devices: a whole 4x4x8 slice. The times are simulated.
256 devices in a mesh: curve: 32 (over x, z), grp: 8 (over y, core).
Axes of the slice: x: 4, y: 4, z: 8, core: 2. Of those that a mesh axis runs over, the one named last changes fastest.
Arguments:
- state: float32 [2, 512, 8, 49152], P(None, None, 'grp', 'curve'), may hold values from -6 to 6
- coef: float32 [512, 8, 49152], P(None, 'grp', 'curve'), may hold values from 0.2 to 4
- counts: int32 [8, 32], P('grp', 'curve'), may hold values from 512 to 1536, as said below
Outputs:
- smoothed: float32 [512, 8, 32768], P(None, 'grp', 'curve')
Inputs may be any that keep to these rules, and one draw needn't show every extreme that they name: `counts`: each rank's count is 1024 plus the drift at its own end minus the drift at the end of the rank before it; drifts lie in -256 to 256, are zero before the first rank and at the last rank, so the curve holds 32768 blocks; in every curve one rank holds exactly 1536 blocks.
All inputs are finite; a program needn't handle non-finite values.
Results may differ from a plain program's by a relative error of at most 0.00002.
Values sent between devices are 32-bit elements; how exact they have to be, the bound alone decides.
A program may use at most 128 MiB of HBM per device.

v0:
```python
import jax
import jax.numpy as jnp
from jax import lax
from jax.experimental import pallas as pl
from jax.experimental.pallas import tpu as pltpu
from jax.sharding import PartitionSpec as P

AVG = 1024
HALF = 256
CAP = 1536
NX, NZ = 4, 8
N_CURVE = NX * NZ
N_GRP = 8
CH = CAP // 128
MESH = pl.DeviceIdType.MESH
ORDER = (2, 3, 4, 5, 1, 6, 0, 7)
GROUPS = ((0, 4), (4, 2), (6, 2))


class Message:
    def __init__(self, make, sends, receives):
        self.make, self.sends, self.receives = make, sends, receives

    def start(self):
        pl.when(self.sends)(lambda: self.make().start())

    def wait_recv(self):
        pl.when(self.receives)(lambda: self.make().wait_recv())

    def wait_send(self):
        pl.when(self.sends)(lambda: self.make().wait_send())


def kernel(
    counts, state, coef, out,
    raw_u, raw_s, raw_c, u0, u1, inv, yh, rx0, rx1, ts0, ts1, ps, pr, ls, lr,
    t2s, t2r, h2s, h2r, wide, flat, cb1, cb2, cb3, cs,
    in_sem, out_sem, send_sem, recv_sem,
):
    rank, grp = lax.axis_index("curve"), lax.axis_index("grp")
    xc, zc = rank // NZ, rank % NZ
    has_left, has_right = rank > 0, rank < N_CURVE - 1
    has_low, has_high = grp > 0, grp < N_GRP - 1
    left, right = (rank + N_CURVE - 1) % N_CURVE, (rank + 1) % N_CURVE
    low, high = (grp + N_GRP - 1) % N_GRP, (grp + 1) % N_GRP

    barrier = pltpu.get_barrier_semaphore()
    peers = [(xc * NZ + (zc + k) % NZ, grp) for k in range(1, NZ)]
    peers += [(((xc + k) % NX) * NZ + zc, grp) for k in range(1, NX)]
    peers += [(r, g) for g in (low, high) for r in (left, rank, right)]
    peers += [(left, grp), (right, grp)]
    for peer in peers:
        pl.semaphore_signal(barrier, inc=1, device_id=peer, device_id_type=MESH)

    loads = {}
    for kind, src, dst in ((0, state.at[0], raw_u), (1, state.at[1], raw_s), (2, coef, raw_c)):
        for x in range(8):
            loads[kind, x] = pltpu.make_async_copy(src.at[x], dst.at[x], in_sem.at[kind, x])
    first_loads = [(0, x) for x in range(8)] + [(1, 0), (1, 7), (2, 0), (2, 7)]
    other_loads = [(kind, x) for x in range(1, 7) for kind in (1, 2)]
    for key in first_loads + other_loads:
        loads[key].start()

    lane = lax.broadcasted_iota(jnp.int32, (8, 128), 1)
    sub = lax.broadcasted_iota(jnp.int32, (8, 128), 0)
    zero = jnp.zeros((8, 128), jnp.float32)
    held = counts[0, 0]

    index = [0]

    def message(src, dst, device, sends, receives):
        at = index[0]
        index[0] += 1

        def make():
            return pltpu.make_async_remote_copy(
                src_ref=src(), dst_ref=dst(), send_sem=send_sem.at[at], recv_sem=recv_sem.at[at],
                device_id=device, device_id_type=MESH,
            )

        return Message(make, sends, receives)

    yes = rank >= 0
    count_z = [
        message(lambda: cs.at[0], lambda: cb1.at[zc], (xc * NZ + (zc + k) % NZ, grp), yes, yes)
        for k in range(1, NZ)
    ]
    count_x = [
        message(lambda: cs.at[1], lambda: cb2.at[xc], (((xc + k) % NX) * NZ + zc, grp), yes, yes)
        for k in range(1, NX)
    ]
    count_g = [
        message(lambda: cs.at[2], lambda: cb3.at[1], (rank, low), has_low, has_high),
        message(lambda: cs.at[2], lambda: cb3.at[0], (rank, high), has_high, has_low),
    ]
    packs = [
        message(lambda: ps.at[0], lambda: pr.at[1], (left, grp), has_left, has_right),
        message(lambda: ps.at[1], lambda: pr.at[0], (right, grp), has_right, has_left),
    ]
    late_packs = [
        message(lambda: ls.at[0], lambda: lr.at[1], (left, grp), has_left, has_right),
        message(lambda: ls.at[1], lambda: lr.at[0], (right, grp), has_right, has_left),
    ]

    def planes_out(u, ts, rx):
        tails, heads, mids = [], [], []
        for d, y, other, sends, receives in (
            (0, 0, low, has_low, has_high), (1, 7, high, has_high, has_low),
        ):
            tails.append(message(
                lambda d=d: ts.at[d], lambda d=d: rx.at[1 - d, :, pl.ds(0, 4)], (right, other),
                jnp.logical_and(sends, has_right), jnp.logical_and(receives, has_left)))
            heads.append(message(
                lambda y=y: u.at[pl.ds(1, 8), y, pl.ds(0, 4)],
                lambda d=d: rx.at[1 - d, :, pl.ds(16, 4)], (left, other),
                jnp.logical_and(sends, has_left), jnp.logical_and(receives, has_right)))
            mids.append(message(
                lambda y=y: u.at[pl.ds(1, 8), y], lambda d=d: rx.at[1 - d, :, pl.ds(4, 12)],
                (rank, other), sends, receives))
        return tails + heads + mids

    planes0 = planes_out(u0, ts0, rx0)
    planes1 = planes_out(u1, ts1, rx1)
    moves = []
    for start, size in GROUPS:
        part = pl.ds(start, size)
        moves.append([
            message(lambda part=part: t2s.at[part], lambda part=part: t2r.at[part], (right, grp),
                    has_right, has_left),
            message(lambda part=part: h2s.at[part], lambda part=part: h2r.at[part], (left, grp),
                    has_left, has_right),
        ])

    def rolled(value, turn):
        return pltpu.roll(value, turn, 1)

    def shifted(load, start, chunks, lowest, highest):
        first, offset = jnp.clip(start >> 7, lowest, highest), start & 127
        turn = (128 - offset) & 127
        turned = {}
        for k in sorted(set(chunks) | {k + 1 for k in chunks}):
            turned[k] = rolled(load(first + k), turn)
        keep = lane < 128 - offset
        return {k: jnp.where(keep, turned[k], turned[k + 1]) for k in chunks}

    def convert(x, carry):
        for y in range(8):
            for c in range(CH):
                u0[x + 1, y, c] = raw_u[x, y, pl.ds(c, 8, stride=CH), :]
        return carry

    def plane_tails(u, ts):
        def body(x, carry):
            for d, y in ((0, 0), (1, 7)):
                got = shifted(
                    lambda k: u[x + 1, y, jnp.minimum(k, CH - 1)], held - 512, range(4), 0, 8)
                for k in range(4):
                    ts[d, x, k] = got[k]
            return carry

        lax.fori_loop(0, 8, body, 0)

    last_chunk, last_lane = jnp.clip((held - 1) >> 7, 0, CH - 1), (held - 1) & 127

    def lanes_packed(load, at, ys):
        acc = zero
        for y in ys:
            acc = jnp.where(lane == y, rolled(load(y), (y - at) & 127) if not isinstance(at, int) else pltpu.roll(load(y), (y - at) & 127, 1), acc)
        return acc

    def first_of(u, x, ys):
        return lanes_packed(lambda y: u[x + 1, y, 0], 0, ys)

    def last_of(u, x, ys):
        return lanes_packed(lambda y: u[x + 1, y, last_chunk], last_lane, ys)

    def fill_x(u, left_tile, right_tile, ys):
        for y in ys:
            from_left = jnp.broadcast_to(left_tile[:, y : y + 1], (8, 128))
            from_right = jnp.broadcast_to(right_tile[:, y : y + 1], (8, 128))
            turned = [pltpu.roll(u[1, y, c], 127, 1) for c in range(CH)]
            for c in range(CH):
                value = jnp.where(lane < 127, turned[c], turned[min(c + 1, CH - 1)])
                u[9, y, c] = jnp.where(lane + 128 * c == held - 1, from_right, value)
            turned = [pltpu.roll(u[8, y, c], 1, 1) for c in range(CH)]
            for c in range(CH):
                u[0, y, c] = jnp.where(lane > 0, turned[c], turned[c - 1] if c else from_left)

    def along_z(value):
        up = jnp.where(sub < 7, pltpu.roll(value, 7, 0), 0.0)
        down = jnp.where(sub > 0, pltpu.roll(value, 1, 0), 0.0)
        return up + down

    def sweep(u, first, ys, store):
        need = sorted({y + d for y in ys for d in (-1, 0, 1)} & set(range(8)))

        def body(x, carry):
            for c in range(CH):
                here = {y: u[x + 1, y, c] for y in need}
                here[-1] = yh[0, x, c] if 0 in ys else None
                here[8] = yh[1, x, c] if 7 in ys else None
                for y in ys:
                    total = u[x, y, c] + u[x + 2, y, c]
                    total = total + (here[y - 1] + here[y + 1]) + along_z(here[y])
                    if first:
                        scale = 1.0 / (6.0 + raw_c[x, y, pl.ds(c, 8, stride=CH), :])
                        inv[x, y, c] = scale
                    else:
                        scale = inv[x, y, c]
                    store(x, y, c, (raw_s[x, y, pl.ds(c, 8, stride=CH), :] + total) * scale)
            return carry

        lax.fori_loop(0, 8, body, 0)

    def store_u1(x, y, c, value):
        u1[x + 1, y, c] = value

    def store_wide(x, y, c, value):
        wide[x, y, c + 2] = value

    def ends(group):
        start, size = GROUPS[group]

        def body(x, carry):
            for p in range(start, start + size):
                y = ORDER[p]
                got = shifted(lambda k: wide[x, y, k + 2], held - HALF, range(2), 2, 10)
                for k in range(2):
                    t2s[p, x, k] = got[k]
                    h2s[p, x, k] = wide[x, y, k + 2]
            return carry

        lax.fori_loop(0, 8, body, 0)

    def halo(rx, side, exists, drift_prev):
        @pl.when(exists)
        def _():
            tile = cb3[side]
            other_prev = tile[0, 0] - rank * AVG
            other_next = tile[1, 0] - (rank + 1) * AVG
            begin = 512 + drift_prev - other_prev
            begin_next = 1024 + drift_prev - other_next

            def body(x, carry):
                load = lambda k: rx[side, x, k]
                own = shifted(load, begin, range(CH), 0, 8)
                later = shifted(load, begin_next, range(4, CH), 4, 12)
                for c in range(CH):
                    value = own[c]
                    if c >= 4:
                        value = jnp.where(lane + 128 * c + drift_prev >= AVG + other_next, later[c], value)
                    yh[side, x, c] = value
                return carry

            lax.fori_loop(0, 8, body, 0)

        @pl.when(jnp.logical_not(exists))
        def _():
            def body(x, carry):
                for c in range(CH):
                    yh[side, x, c] = zero
                return carry

            lax.fori_loop(0, 8, body, 0)

    def y_parts(group):
        return ((pl.ds(2, 4),), (pl.ds(1, 1), pl.ds(6, 1)), (pl.ds(0, 1), pl.ds(7, 1)))[group]

    results = []
    for group in range(3):
        results.append([
            pltpu.make_async_copy(
                flat.at[:, part], out.at[:, part], out_sem.at[group, i])
            for i, part in enumerate(y_parts(group))
        ])

    def finish(group, drift_prev, drift_next):
        for move in moves[group]:
            move.wait_recv()
        start, size = GROUPS[group]

        def body(x, carry):
            for p in range(start, start + size):
                y = ORDER[p]
                for k in range(2):
                    wide[x, y, k] = t2r[p, x, k]
                    wide[x, y, 14 + k] = h2r[p, x, k]
                load = lambda k: wide[x, y, k]
                own = shifted(load, HALF - drift_prev, range(8), 0, 4)
                later = shifted(load, 768 - drift_next, range(6, 8), 4, 8)
                for k in range(8):
                    value = own[k]
                    if k >= 6:
                        value = jnp.where(lane + 128 * k >= AVG + drift_next, later[k], value)
                    flat[x, y, pl.ds(k, 8, stride=8), :] = value
            return carry

        lax.fori_loop(0, 8, body, 0)
        for result in results[group]:
            result.start()

    for key in first_loads[:8]:
        loads[key].wait()
    lax.fori_loop(0, 8, convert, 0)
    cs[0] = jnp.full((8, 128), held, jnp.int32)
    cb1[zc] = jnp.full((8, 128), held, jnp.int32)
    plane_tails(u0, ts0)
    for key in first_loads[8:]:
        loads[key].wait()
    every = range(8)
    ps[0, 0] = first_of(u0, 0, every)
    ps[0, 1] = first_of(u0, 1, every)
    ps[1, 0] = last_of(u0, 7, every)
    ps[1, 1] = last_of(u0, 6, every)
    for k, raw in ((2, raw_s), (3, raw_c)):
        ps[0, k] = lanes_packed(lambda y: raw[0, y, pl.ds(0, 8, stride=CH), :], 0, every)

        def last_tile(y):
            tile = raw[7, y, pl.ds(0, 8, stride=CH), :]
            for c in range(1, CH):
                tile = jnp.where(last_chunk == c, raw[7, y, pl.ds(c, 8, stride=CH), :], tile)
            return tile

        ps[1, k] = lanes_packed(last_tile, last_lane, every)

    pl.semaphore_wait(barrier, len(peers))
    for m in packs + count_z + planes0:
        m.start()

    for key in other_loads:
        loads[key].wait()
    for m in packs:
        m.wait_recv()
    left0 = jnp.where(has_left, pr[0, 0], zero)
    right0 = jnp.where(has_right, pr[1, 0], zero)
    fill_x(u0, left0, right0, every)
    sweep(u0, True, range(1, 7), store_u1)

    def edge_u1(side, own, exists):
        u = pr[side, 0]
        along_y = jnp.where(lane < 7, pltpu.roll(u, 127, 1), 0.0) + jnp.where(lane > 0, pltpu.roll(u, 1, 1), 0.0)
        total = pr[side, 1] + own + along_y + along_z(u)
        return jnp.where(exists, (pr[side, 2] + total) / (6.0 + pr[side, 3]), zero)

    left1 = edge_u1(0, ps[0, 0], has_left)
    right1 = edge_u1(1, ps[1, 0], has_right)
    fill_x(u1, left1, right1, range(1, 7))

    for m in count_z:
        m.wait_recv()
    line = jnp.zeros((8, 128), jnp.int32)
    before = line
    for z in range(NZ):
        tile = cb1[z]
        line = line + tile
        before = before + jnp.where(z < zc, tile, 0)
    cs[1] = line
    cb2[xc] = line
    for m in count_x:
        m.start()

    sweep(u1, False, range(2, 6), store_wide)
    ends(0)
    for m in moves[0]:
        m.start()

    for m in count_x:
        m.wait_recv()
    for x in range(NX):
        before = before + jnp.where(x < xc, cb2[x], 0)
    cs[2] = jnp.where(sub == 0, before, before + held)
    for m in count_g:
        m.start()
    drift_prev = before[0, 0] - rank * AVG
    drift_next = drift_prev + held - AVG

    for m in planes0 + count_g:
        m.wait_recv()
    halo(rx0, 0, has_low, drift_prev)
    halo(rx0, 1, has_high, drift_prev)
    sweep(u0, True, (0, 7), store_u1)
    plane_tails(u1, ts1)
    ls[0] = first_of(u1, 0, (0, 7))
    ls[1] = last_of(u1, 7, (0, 7))
    for m in late_packs + planes1:
        m.start()

    sweep(u1, False, (1, 6), store_wide)
    ends(1)
    for m in moves[1]:
        m.start()
    finish(0, drift_prev, drift_next)

    for m in late_packs:
        m.wait_recv()
    fill_x(u1, jnp.where(has_left, lr[0], zero), jnp.where(has_right, lr[1], zero), (0, 7))
    for m in planes1:
        m.wait_recv()
    halo(rx1, 0, has_low, drift_prev)
    halo(rx1, 1, has_high, drift_prev)
    sweep(u1, False, (0, 7), store_wide)
    ends(2)
    for m in moves[2]:
        m.start()
    finish(1, drift_prev, drift_next)
    finish(2, drift_prev, drift_next)

    for m in packs + count_z + planes0 + count_x + count_g + late_packs + planes1:
        m.wait_send()
    for pair in moves:
        for m in pair:
            m.wait_send()
    for group in results:
        for result in group:
            result.wait()


N_MESSAGES = (NZ - 1) + (NX - 1) + 2 + 2 + 2 + 6 + 6 + 6


def local(state, coef, counts):
    f32, i32 = jnp.float32, jnp.int32
    vmem = pltpu.VMEM
    result = pl.pallas_call(
        kernel,
        out_shape=jax.ShapeDtypeStruct((8, 8, 64, 128), f32),
        in_specs=[
            pl.BlockSpec(memory_space=pltpu.SMEM),
            pl.BlockSpec(memory_space=pl.ANY),
            pl.BlockSpec(memory_space=pl.ANY),
        ],
        out_specs=pl.BlockSpec(memory_space=pl.ANY),
        scratch_shapes=[
            vmem((8, 8, 96, 128), f32), vmem((8, 8, 96, 128), f32), vmem((8, 8, 96, 128), f32),
            vmem((10, 8, CH, 8, 128), f32), vmem((10, 8, CH, 8, 128), f32), vmem((8, 8, CH, 8, 128), f32),
            vmem((2, 8, CH, 8, 128), f32),
            vmem((2, 8, 25, 8, 128), f32), vmem((2, 8, 25, 8, 128), f32),
            vmem((2, 8, 4, 8, 128), f32), vmem((2, 8, 4, 8, 128), f32),
            vmem((2, 4, 8, 128), f32), vmem((2, 4, 8, 128), f32),
            vmem((2, 8, 128), f32), vmem((2, 8, 128), f32),
            vmem((8, 8, 2, 8, 128), f32), vmem((8, 8, 2, 8, 128), f32),
            vmem((8, 8, 2, 8, 128), f32), vmem((8, 8, 2, 8, 128), f32),
            vmem((8, 8, 17, 8, 128), f32), vmem((8, 8, 64, 128), f32),
            vmem((NZ, 8, 128), i32), vmem((NX, 8, 128), i32), vmem((2, 8, 128), i32), vmem((3, 8, 128), i32),
            pltpu.SemaphoreType.DMA((3, 8)), pltpu.SemaphoreType.DMA((3, 2)),
            pltpu.SemaphoreType.DMA((N_MESSAGES,)), pltpu.SemaphoreType.DMA((N_MESSAGES,)),
        ],
        compiler_params=pltpu.CompilerParams(
            collective_id=0, has_side_effects=True, vmem_limit_bytes=60 * 1024 * 1024),
    )(counts, state.reshape(2, 8, 8, 96, 128), coef.reshape(8, 8, 96, 128))
    return result.reshape(512, 1, AVG)


def solution(mesh):
    placed = (P(None, None, "grp", "curve"), P(None, "grp", "curve"), P("grp", "curve"))
    return jax.shard_map(
        local, mesh=mesh, in_specs=placed, out_specs=P(None, "grp", "curve"), check_vma=False
    )
```

profile of v0, /device:TPU:18, one launch (start us, length us, event | category | flops | bytes accessed | tf_op | source)
XLA Modules:
  0.0 50.4 jit_solution(2612848642743611182)
XLA Ops:
  0.7 45.4 %shard_map.37 = f32[8,8,64,128]{3,2,1,0:T(8,128)} custom-call(s32[1,1]{1,0:T(1,128)S(6)} %copy.6.counts, f32[2,8,8,96,128]{4,3,2,1,0:T(8,128)} %bitcast.4, f32[8,8,96,128]{3,2,1,0:T(8,128)} %bitcast.5), custom_call_target="tpu_custom_call" | custom-call | tf_op jit(solution)/shard_map/pallas_call | solution.py:424
  46.0 4.3 %copy.7 = f32[512,1,1024]{2,1,0:T(1,128)} copy(f32[512,1,1024]{2,1,0:T(1,128)} %bitcast.3) | data formatting | bytes 4194304
where the time goes:
time: 51.2 us; the launch traced here: 50.4 us
  Pallas kernels  45.4 us (89%)
  local copies, waits for them, and re-layouts  4.35 us (8%)
  between operations  0.66 us (1%)
    pallas_call x1, Pallas kernels, local(): pl.pallas_call(kernel, out_shape=jax.ShapeDtypeStruct((8, 8, 64, 128), f3...  45.4 us
    unnamed x1, local copies, waits for them, and re-layouts  4.35 us

commit v1 on v0

--- a/solution.py
+++ b/solution.py
@@ -8,8 +8,7 @@
 AVG = 1024
 HALF = 256
 CAP = 1536
-NX, NZ = 4, 8
-N_CURVE = NX * NZ
+N_CURVE = 32
 N_GRP = 8
 CH = CAP // 128
 MESH = pl.DeviceIdType.MESH
@@ -34,21 +33,18 @@
 def kernel(
     counts, state, coef, out,
     raw_u, raw_s, raw_c, u0, u1, inv, yh, rx0, rx1, ts0, ts1, ps, pr, ls, lr,
-    t2s, t2r, h2s, h2r, wide, flat, cb1, cb2, cb3, cs,
-    in_sem, out_sem, send_sem, recv_sem,
+    t2s, t2r, h2s, h2r, wide, cb, cb3, cs, cs3,
+    in_sem, send_sem, recv_sem,
 ):
     rank, grp = lax.axis_index("curve"), lax.axis_index("grp")
-    xc, zc = rank // NZ, rank % NZ
     has_left, has_right = rank > 0, rank < N_CURVE - 1
     has_low, has_high = grp > 0, grp < N_GRP - 1
     left, right = (rank + N_CURVE - 1) % N_CURVE, (rank + 1) % N_CURVE
     low, high = (grp + N_GRP - 1) % N_GRP, (grp + 1) % N_GRP
 
     barrier = pltpu.get_barrier_semaphore()
-    peers = [(xc * NZ + (zc + k) % NZ, grp) for k in range(1, NZ)]
-    peers += [(((xc + k) % NX) * NZ + zc, grp) for k in range(1, NX)]
-    peers += [(r, g) for g in (low, high) for r in (left, rank, right)]
-    peers += [(left, grp), (right, grp)]
+    peers = [(r, g) for g in (low, high) for r in (left, rank, right)]
+    peers += [((rank + k) % N_CURVE, grp) for k in range(1, N_CURVE)]
     for peer in peers:
         pl.semaphore_signal(barrier, inc=1, device_id=peer, device_id_type=MESH)
 
@@ -58,7 +54,7 @@
             loads[kind, x] = pltpu.make_async_copy(src.at[x], dst.at[x], in_sem.at[kind, x])
     first_loads = [(0, x) for x in range(8)] + [(1, 0), (1, 7), (2, 0), (2, 7)]
     other_loads = [(kind, x) for x in range(1, 7) for kind in (1, 2)]
-    for key in first_loads + other_loads:
+    for key in first_loads:
         loads[key].start()
 
     lane = lax.broadcasted_iota(jnp.int32, (8, 128), 1)
@@ -81,17 +77,13 @@
         return Message(make, sends, receives)
 
     yes = rank >= 0
-    count_z = [
-        message(lambda: cs.at[0], lambda: cb1.at[zc], (xc * NZ + (zc + k) % NZ, grp), yes, yes)
-        for k in range(1, NZ)
-    ]
-    count_x = [
-        message(lambda: cs.at[1], lambda: cb2.at[xc], (((xc + k) % NX) * NZ + zc, grp), yes, yes)
-        for k in range(1, NX)
+    count_all = [
+        message(lambda: cs, lambda: cb.at[rank], ((rank + k) % N_CURVE, grp), yes, yes)
+        for k in range(1, N_CURVE)
     ]
     count_g = [
-        message(lambda: cs.at[2], lambda: cb3.at[1], (rank, low), has_low, has_high),
-        message(lambda: cs.at[2], lambda: cb3.at[0], (rank, high), has_high, has_low),
+        message(lambda: cs3, lambda: cb3.at[1], (rank, low), has_low, has_high),
+        message(lambda: cs3, lambda: cb3.at[0], (rank, high), has_high, has_low),
     ]
     packs = [
         message(lambda: ps.at[0], lambda: pr.at[1], (left, grp), has_left, has_right),
@@ -131,6 +123,19 @@
                     has_left, has_right),
         ])
 
+    def loop(start, stop, body, unroll=1):
+        if unroll == stop - start:
+            for x in range(start, stop):
+                body(x)
+            return
+
+        def step(i, carry):
+            for k in range(unroll):
+                body(start + i * unroll + k)
+            return carry
+
+        lax.fori_loop(0, (stop - start) // unroll, step, 0)
+
     def rolled(value, turn):
         return pltpu.roll(value, turn, 1)
 
@@ -143,22 +148,20 @@
         keep = lane < 128 - offset
         return {k: jnp.where(keep, turned[k], turned[k + 1]) for k in chunks}
 
-    def convert(x, carry):
+    def convert(x):
         for y in range(8):
             for c in range(CH):
                 u0[x + 1, y, c] = raw_u[x, y, pl.ds(c, 8, stride=CH), :]
-        return carry
 
     def plane_tails(u, ts):
-        def body(x, carry):
+        def body(x):
             for d, y in ((0, 0), (1, 7)):
                 got = shifted(
                     lambda k: u[x + 1, y, jnp.minimum(k, CH - 1)], held - 512, range(4), 0, 8)
                 for k in range(4):
                     ts[d, x, k] = got[k]
-            return carry
-
-        lax.fori_loop(0, 8, body, 0)
+
+        loop(0, 8, body, 8)
 
     last_chunk, last_lane = jnp.clip((held - 1) >> 7, 0, CH - 1), (held - 1) & 127
 
@@ -191,10 +194,10 @@
         down = jnp.where(sub > 0, pltpu.roll(value, 1, 0), 0.0)
         return up + down
 
-    def sweep(u, first, ys, store):
+    def sweep(u, first, ys, store, xs=(0, 8, 1)):
         need = sorted({y + d for y in ys for d in (-1, 0, 1)} & set(range(8)))
 
-        def body(x, carry):
+        def body(x):
             for c in range(CH):
                 here = {y: u[x + 1, y, c] for y in need}
                 here[-1] = yh[0, x, c] if 0 in ys else None
@@ -208,9 +211,8 @@
                     else:
                         scale = inv[x, y, c]
                     store(x, y, c, (raw_s[x, y, pl.ds(c, 8, stride=CH), :] + total) * scale)
-            return carry
-
-        lax.fori_loop(0, 8, body, 0)
+
+        loop(xs[0], xs[1], body, xs[2])
 
     def store_u1(x, y, c, value):
         u1[x + 1, y, c] = value
@@ -221,65 +223,44 @@
     def ends(group):
         start, size = GROUPS[group]
 
-        def body(x, carry):
+        def body(x):
             for p in range(start, start + size):
                 y = ORDER[p]
                 got = shifted(lambda k: wide[x, y, k + 2], held - HALF, range(2), 2, 10)
                 for k in range(2):
                     t2s[p, x, k] = got[k]
                     h2s[p, x, k] = wide[x, y, k + 2]
-            return carry
-
-        lax.fori_loop(0, 8, body, 0)
-
-    def halo(rx, side, exists, drift_prev):
-        @pl.when(exists)
-        def _():
+
+        loop(0, 8, body, 8)
+
+    def halos(rx, drift_prev):
+        starts = []
+        for side in range(2):
             tile = cb3[side]
             other_prev = tile[0, 0] - rank * AVG
             other_next = tile[1, 0] - (rank + 1) * AVG
-            begin = 512 + drift_prev - other_prev
-            begin_next = 1024 + drift_prev - other_next
-
-            def body(x, carry):
+            starts.append((AVG // 2 + drift_prev - other_prev, AVG + drift_prev - other_next))
+
+        def body(x):
+            for side, exists in ((0, has_low), (1, has_high)):
                 load = lambda k: rx[side, x, k]
+                begin, begin_next = starts[side]
                 own = shifted(load, begin, range(CH), 0, 8)
                 later = shifted(load, begin_next, range(4, CH), 4, 12)
                 for c in range(CH):
                     value = own[c]
                     if c >= 4:
-                        value = jnp.where(lane + 128 * c + drift_prev >= AVG + other_next, later[c], value)
-                    yh[side, x, c] = value
-                return carry
-
-            lax.fori_loop(0, 8, body, 0)
-
-        @pl.when(jnp.logical_not(exists))
-        def _():
-            def body(x, carry):
-                for c in range(CH):
-                    yh[side, x, c] = zero
-                return carry
-
-            lax.fori_loop(0, 8, body, 0)
-
-    def y_parts(group):
-        return ((pl.ds(2, 4),), (pl.ds(1, 1), pl.ds(6, 1)), (pl.ds(0, 1), pl.ds(7, 1)))[group]
-
-    results = []
-    for group in range(3):
-        results.append([
-            pltpu.make_async_copy(
-                flat.at[:, part], out.at[:, part], out_sem.at[group, i])
-            for i, part in enumerate(y_parts(group))
-        ])
+                        value = jnp.where(lane + 128 * c >= 2 * AVG - begin_next, later[c], value)
+                    yh[side, x, c] = jnp.where(exists, value, zero)
+
+        loop(0, 8, body, 4)
 
     def finish(group, drift_prev, drift_next):
         for move in moves[group]:
             move.wait_recv()
         start, size = GROUPS[group]
 
-        def body(x, carry):
+        def body(x):
             for p in range(start, start + size):
                 y = ORDER[p]
                 for k in range(2):
@@ -292,18 +273,16 @@
                     value = own[k]
                     if k >= 6:
                         value = jnp.where(lane + 128 * k >= AVG + drift_next, later[k], value)
-                    flat[x, y, pl.ds(k, 8, stride=8), :] = value
-            return carry
-
-        lax.fori_loop(0, 8, body, 0)
-        for result in results[group]:
-            result.start()
+                    out[x, y, pl.ds(k, 8, stride=8), :] = value
+
+        loop(0, 8, body, 8 // size)
 
     for key in first_loads[:8]:
         loads[key].wait()
-    lax.fori_loop(0, 8, convert, 0)
-    cs[0] = jnp.full((8, 128), held, jnp.int32)
-    cb1[zc] = jnp.full((8, 128), held, jnp.int32)
+    for key in other_loads:
+        loads[key].start()
+    loop(0, 8, convert)
+    cs[...] = jnp.full((1, 128), held, jnp.int32)
     plane_tails(u0, ts0)
     for key in first_loads[8:]:
         loads[key].wait()
@@ -324,17 +303,19 @@
         ps[1, k] = lanes_packed(last_tile, last_lane, every)
 
     pl.semaphore_wait(barrier, len(peers))
-    for m in packs + count_z + planes0:
+    for m in packs + count_all + planes0:
         m.start()
 
     for key in other_loads:
         loads[key].wait()
+    sweep(u0, True, range(1, 7), store_u1, (1, 7, 1))
     for m in packs:
         m.wait_recv()
     left0 = jnp.where(has_left, pr[0, 0], zero)
     right0 = jnp.where(has_right, pr[1, 0], zero)
     fill_x(u0, left0, right0, every)
-    sweep(u0, True, range(1, 7), store_u1)
+    sweep(u0, True, range(1, 7), store_u1, (0, 1, 1))
+    sweep(u0, True, range(1, 7), store_u1, (7, 8, 1))
 
     def edge_u1(side, own, exists):
         u = pr[side, 0]
@@ -345,39 +326,25 @@
     left1 = edge_u1(0, ps[0, 0], has_left)
     right1 = edge_u1(1, ps[1, 0], has_right)
     fill_x(u1, left1, right1, range(1, 7))
-
-    for m in count_z:
-        m.wait_recv()
-    line = jnp.zeros((8, 128), jnp.int32)
-    before = line
-    for z in range(NZ):
-        tile = cb1[z]
-        line = line + tile
-        before = before + jnp.where(z < zc, tile, 0)
-    cs[1] = line
-    cb2[xc] = line
-    for m in count_x:
-        m.start()
-
     sweep(u1, False, range(2, 6), store_wide)
     ends(0)
     for m in moves[0]:
         m.start()
 
-    for m in count_x:
+    for m in count_all:
         m.wait_recv()
-    for x in range(NX):
-        before = before + jnp.where(x < xc, cb2[x], 0)
-    cs[2] = jnp.where(sub == 0, before, before + held)
-    for m in count_g:
-        m.start()
+    before = jnp.zeros((1, 128), jnp.int32)
+    for r in range(N_CURVE - 1):
+        before = before + jnp.where(r < rank, cb[r], 0)
     drift_prev = before[0, 0] - rank * AVG
     drift_next = drift_prev + held - AVG
+    cs3[...] = jnp.where(sub == 0, before, before + held)
+    for m in count_g:
+        m.start()
 
     for m in planes0 + count_g:
         m.wait_recv()
-    halo(rx0, 0, has_low, drift_prev)
-    halo(rx0, 1, has_high, drift_prev)
+    halos(rx0, drift_prev)
     sweep(u0, True, (0, 7), store_u1)
     plane_tails(u1, ts1)
     ls[0] = first_of(u1, 0, (0, 7))
@@ -396,8 +363,7 @@
     fill_x(u1, jnp.where(has_left, lr[0], zero), jnp.where(has_right, lr[1], zero), (0, 7))
     for m in planes1:
         m.wait_recv()
-    halo(rx1, 0, has_low, drift_prev)
-    halo(rx1, 1, has_high, drift_prev)
+    halos(rx1, drift_prev)
     sweep(u1, False, (0, 7), store_wide)
     ends(2)
     for m in moves[2]:
@@ -405,17 +371,14 @@
     finish(1, drift_prev, drift_next)
     finish(2, drift_prev, drift_next)
 
-    for m in packs + count_z + planes0 + count_x + count_g + late_packs + planes1:
+    for m in packs + count_all + planes0 + count_g + late_packs + planes1:
         m.wait_send()
     for pair in moves:
         for m in pair:
             m.wait_send()
-    for group in results:
-        for result in group:
-            result.wait()
-
-
-N_MESSAGES = (NZ - 1) + (NX - 1) + 2 + 2 + 2 + 6 + 6 + 6
+
+
+N_MESSAGES = (N_CURVE - 1) + 2 + 2 + 2 + 6 + 6 + 6
 
 
 def local(state, coef, counts):
@@ -423,13 +386,13 @@
     vmem = pltpu.VMEM
     result = pl.pallas_call(
         kernel,
-        out_shape=jax.ShapeDtypeStruct((8, 8, 64, 128), f32),
+        out_shape=vmem((8, 8, 64, 128), f32),
         in_specs=[
             pl.BlockSpec(memory_space=pltpu.SMEM),
             pl.BlockSpec(memory_space=pl.ANY),
             pl.BlockSpec(memory_space=pl.ANY),
         ],
-        out_specs=pl.BlockSpec(memory_space=pl.ANY),
+        out_specs=pl.BlockSpec(memory_space=vmem),
         scratch_shapes=[
             vmem((8, 8, 96, 128), f32), vmem((8, 8, 96, 128), f32), vmem((8, 8, 96, 128), f32),
             vmem((10, 8, CH, 8, 128), f32), vmem((10, 8, CH, 8, 128), f32), vmem((8, 8, CH, 8, 128), f32),
@@ -440,9 +403,9 @@
             vmem((2, 8, 128), f32), vmem((2, 8, 128), f32),
             vmem((8, 8, 2, 8, 128), f32), vmem((8, 8, 2, 8, 128), f32),
             vmem((8, 8, 2, 8, 128), f32), vmem((8, 8, 2, 8, 128), f32),
-            vmem((8, 8, 17, 8, 128), f32), vmem((8, 8, 64, 128), f32),
-            vmem((NZ, 8, 128), i32), vmem((NX, 8, 128), i32), vmem((2, 8, 128), i32), vmem((3, 8, 128), i32),
-            pltpu.SemaphoreType.DMA((3, 8)), pltpu.SemaphoreType.DMA((3, 2)),
+            vmem((8, 8, 17, 8, 128), f32),
+            vmem((N_CURVE, 1, 128), i32), vmem((2, 8, 128), i32), vmem((1, 128), i32), vmem((8, 128), i32),
+            pltpu.SemaphoreType.DMA((3, 8)),
             pltpu.SemaphoreType.DMA((N_MESSAGES,)), pltpu.SemaphoreType.DMA((N_MESSAGES,)),
         ],
         compiler_params=pltpu.CompilerParams(

time: 51.2 us -> 39.8 us (0.78); the launches traced: 50.4 us -> 39.7 us
  Pallas kernels: 45.4 us -> 37.7 us
  local copies, waits for them, and re-layouts: 4.35 us -> 1.32 us
    pallas_call x1, Pallas kernels: 45.4 us -> 37.7 us  [local(): pl.pallas_call(kernel, out_shape=vmem((8, 8, 64, 128), f32), in_specs=[pl...]
    unnamed x1, local copies, waits for them, and re-layouts: 4.35 us -> 1.32 us
where the time goes in v1:
time: 39.8 us; the launch traced here: 39.7 us
  Pallas kernels  37.7 us (95%)
  local copies, waits for them, and re-layouts  1.32 us (3%)
  between operations  0.66 us (2%)
    pallas_call x1, Pallas kernels, local(): pl.pallas_call(kernel, out_shape=vmem((8, 8, 64, 128), f32), in_specs=[pl...  37.7 us
    unnamed x1, local copies, waits for them, and re-layouts  1.32 us

profile of v1, /device:TPU:18, one launch (start us, length us, event | category | flops | bytes accessed | tf_op | source)
XLA Modules:
  0.0 39.7 jit_solution(1431701816391939607)
XLA Ops:
  0.7 37.7 %shard_map.37 = f32[8,8,64,128]{3,2,1,0:T(8,128)S(1)} custom-call(s32[1,1]{1,0:T(1,128)S(6)} %copy.7.counts, f32[2,8,8,96,128]{4,3,2,1,0:T(8,128)} %bitcast.4, f32[8,8,96,128]{3,2,1,0:T(8,128)} %bitcast.5), custom_call_target="tpu_custom_call" | custom-call | tf_op jit(solution)/shard_map/pallas_call | solution.py:387
  38.4 1.3 %copy.6 = f32[512,1,1024]{2,1,0:T(1,128)} copy(f32[512,1,1024]{2,1,0:T(1,128)S(1)} %bitcast.3) | data formatting | bytes 4194304

commit v2 on v1

--- a/solution.py
+++ b/solution.py
@@ -8,12 +8,15 @@
 AVG = 1024
 HALF = 256
 CAP = 1536
-N_CURVE = 32
+NX, NZ = 4, 8
+N_CURVE = NX * NZ
 N_GRP = 8
 CH = CAP // 128
 MESH = pl.DeviceIdType.MESH
 ORDER = (2, 3, 4, 5, 1, 6, 0, 7)
-GROUPS = ((0, 4), (4, 2), (6, 2))
+INNER, EDGE_LOW, EDGE_HIGH, NEXT, LAST_LOW, LAST_HIGH = PARTS = (
+    (0, 4, 2, 4), (0, 4, 0, 2), (0, 4, 6, 2), (4, 2, 0, 8), (6, 1, 0, 8), (7, 1, 0, 8),
+)
 
 
 class Message:
@@ -33,10 +36,12 @@
 def kernel(
     counts, state, coef, out,
     raw_u, raw_s, raw_c, u0, u1, inv, yh, rx0, rx1, ts0, ts1, ps, pr, ls, lr,
-    t2s, t2r, h2s, h2r, wide, cb, cb3, cs, cs3,
+    t2s, t2r, h2s, h2r, wide, cbx, cbz, cb3, cs, cs3,
+
     in_sem, send_sem, recv_sem,
 ):
     rank, grp = lax.axis_index("curve"), lax.axis_index("grp")
+    xc, zc = rank // NZ, rank % NZ
     has_left, has_right = rank > 0, rank < N_CURVE - 1
     has_low, has_high = grp > 0, grp < N_GRP - 1
     left, right = (rank + N_CURVE - 1) % N_CURVE, (rank + 1) % N_CURVE
@@ -44,10 +49,9 @@
 
     barrier = pltpu.get_barrier_semaphore()
     peers = [(r, g) for g in (low, high) for r in (left, rank, right)]
-    peers += [((rank + k) % N_CURVE, grp) for k in range(1, N_CURVE)]
-    for peer in peers:
-        pl.semaphore_signal(barrier, inc=1, device_id=peer, device_id_type=MESH)
-
+    peers += [(left, grp), (right, grp)]
+    peers += [(((xc + k) % NX) * NZ + zc, grp) for k in range(1, NX)]
+    peers += [(xc * NZ + (zc + k) % NZ, grp) for k in range(1, NZ)]
     loads = {}
     for kind, src, dst in ((0, state.at[0], raw_u), (1, state.at[1], raw_s), (2, coef, raw_c)):
         for x in range(8):
@@ -56,6 +60,8 @@
     other_loads = [(kind, x) for x in range(1, 7) for kind in (1, 2)]
     for key in first_loads:
         loads[key].start()
+    for peer in peers:
+        pl.semaphore_signal(barrier, inc=1, device_id=peer, device_id_type=MESH)
 
     lane = lax.broadcasted_iota(jnp.int32, (8, 128), 1)
     sub = lax.broadcasted_iota(jnp.int32, (8, 128), 0)
@@ -77,9 +83,13 @@
         return Message(make, sends, receives)
 
     yes = rank >= 0
-    count_all = [
-        message(lambda: cs, lambda: cb.at[rank], ((rank + k) % N_CURVE, grp), yes, yes)
-        for k in range(1, N_CURVE)
+    count_x = [
+        message(lambda: cs, lambda: cbx.at[xc], (((xc + k) % NX) * NZ + zc, grp), yes, yes)
+        for k in range(1, NX)
+    ]
+    count_z = [
+        message(lambda: cbx, lambda: cbz.at[zc], (xc * NZ + (zc + k) % NZ, grp), yes, yes)
+        for k in range(1, NZ)
     ]
     count_g = [
         message(lambda: cs3, lambda: cb3.at[1], (rank, low), has_low, has_high),
@@ -109,19 +119,19 @@
             mids.append(message(
                 lambda y=y: u.at[pl.ds(1, 8), y], lambda d=d: rx.at[1 - d, :, pl.ds(4, 12)],
                 (rank, other), sends, receives))
-        return tails + heads + mids
-
-    planes0 = planes_out(u0, ts0, rx0)
-    planes1 = planes_out(u1, ts1, rx1)
-    moves = []
-    for start, size in GROUPS:
-        part = pl.ds(start, size)
-        moves.append([
-            message(lambda part=part: t2s.at[part], lambda part=part: t2r.at[part], (right, grp),
-                    has_right, has_left),
-            message(lambda part=part: h2s.at[part], lambda part=part: h2r.at[part], (left, grp),
-                    has_left, has_right),
-        ])
+        return [tails[0], heads[0]], mids, [tails[1], heads[1]]
+
+    planes0_low, planes0_mid, planes0_high = planes_out(u0, ts0, rx0)
+    planes0 = planes0_low + planes0_mid + planes0_high
+    planes1_low, planes1_mid, planes1_high = planes_out(u1, ts1, rx1)
+    planes1 = planes1_low + planes1_high + planes1_mid
+    moves = {}
+    for part in PARTS:
+        at = (pl.ds(part[0], part[1]), pl.ds(part[2], part[3]))
+        moves[part] = [
+            message(lambda at=at: t2s.at[at], lambda at=at: t2r.at[at], (right, grp), has_right, has_left),
+            message(lambda at=at: h2s.at[at], lambda at=at: h2r.at[at], (left, grp), has_left, has_right),
+        ]
 
     def loop(start, stop, body, unroll=1):
         if unroll == stop - start:
@@ -220,8 +230,8 @@
     def store_wide(x, y, c, value):
         wide[x, y, c + 2] = value
 
-    def ends(group):
-        start, size = GROUPS[group]
+    def move(part):
+        start, size, x_start, x_size = part
 
         def body(x):
             for p in range(start, start + size):
@@ -231,7 +241,7 @@
                     t2s[p, x, k] = got[k]
                     h2s[p, x, k] = wide[x, y, k + 2]
 
-        loop(0, 8, body, 8)
+        loop(x_start, x_start + x_size, body, x_size)
 
     def halos(rx, drift_prev):
         starts = []
@@ -255,10 +265,10 @@
 
         loop(0, 8, body, 4)
 
-    def finish(group, drift_prev, drift_next):
-        for move in moves[group]:
-            move.wait_recv()
-        start, size = GROUPS[group]
+    def finish(part, drift_prev, drift_next):
+        for m in moves[part]:
+            m.wait_recv()
+        start, size, x_start, x_size = part
 
         def body(x):
             for p in range(start, start + size):
@@ -275,7 +285,7 @@
                         value = jnp.where(lane + 128 * k >= AVG + drift_next, later[k], value)
                     out[x, y, pl.ds(k, 8, stride=8), :] = value
 
-        loop(0, 8, body, 8 // size)
+        loop(x_start, x_start + x_size, body, min(x_size, 8 // size))
 
     for key in first_loads[:8]:
         loads[key].wait()
@@ -283,6 +293,7 @@
         loads[key].start()
     loop(0, 8, convert)
     cs[...] = jnp.full((1, 128), held, jnp.int32)
+    cbx[xc] = jnp.full((1, 128), held, jnp.int32)
     plane_tails(u0, ts0)
     for key in first_loads[8:]:
         loads[key].wait()
@@ -303,12 +314,18 @@
         ps[1, k] = lanes_packed(last_tile, last_lane, every)
 
     pl.semaphore_wait(barrier, len(peers))
-    for m in packs + count_all + planes0:
+    for m in packs + count_x + planes0_low + planes0_mid:
         m.start()
 
     for key in other_loads:
         loads[key].wait()
     sweep(u0, True, range(1, 7), store_u1, (1, 7, 1))
+    sweep(u1, False, range(2, 6), store_wide, (2, 6, 1))
+    move(INNER)
+    for m in count_x:
+        m.wait_recv()
+    for m in count_z + planes0_high + moves[INNER]:
+        m.start()
     for m in packs:
         m.wait_recv()
     left0 = jnp.where(has_left, pr[0, 0], zero)
@@ -326,16 +343,20 @@
     left1 = edge_u1(0, ps[0, 0], has_left)
     right1 = edge_u1(1, ps[1, 0], has_right)
     fill_x(u1, left1, right1, range(1, 7))
-    sweep(u1, False, range(2, 6), store_wide)
-    ends(0)
-    for m in moves[0]:
-        m.start()
-
-    for m in count_all:
+    sweep(u1, False, range(2, 6), store_wide, (0, 2, 1))
+    move(EDGE_LOW)
+    for m in moves[EDGE_LOW]:
+        m.start()
+    sweep(u1, False, range(2, 6), store_wide, (6, 8, 1))
+    move(EDGE_HIGH)
+
+    for m in count_z:
         m.wait_recv()
     before = jnp.zeros((1, 128), jnp.int32)
-    for r in range(N_CURVE - 1):
-        before = before + jnp.where(r < rank, cb[r], 0)
+    for x in range(NX):
+        for z in range(NZ):
+            row = jnp.where(z == zc, cbx[x], cbz[z, x])
+            before = before + jnp.where(x * NZ + z < rank, row, 0)
     drift_prev = before[0, 0] - rank * AVG
     drift_next = drift_prev + held - AVG
     cs3[...] = jnp.where(sub == 0, before, before + held)
@@ -349,14 +370,15 @@
     plane_tails(u1, ts1)
     ls[0] = first_of(u1, 0, (0, 7))
     ls[1] = last_of(u1, 7, (0, 7))
-    for m in late_packs + planes1:
+    for m in late_packs + planes1 + moves[EDGE_HIGH]:
         m.start()
 
     sweep(u1, False, (1, 6), store_wide)
-    ends(1)
-    for m in moves[1]:
-        m.start()
-    finish(0, drift_prev, drift_next)
+    move(NEXT)
+    for m in moves[NEXT]:
+        m.start()
+    finish(INNER, drift_prev, drift_next)
+    finish(EDGE_LOW, drift_prev, drift_next)
 
     for m in late_packs:
         m.wait_recv()
@@ -365,20 +387,21 @@
         m.wait_recv()
     halos(rx1, drift_prev)
     sweep(u1, False, (0, 7), store_wide)
-    ends(2)
-    for m in moves[2]:
-        m.start()
-    finish(1, drift_prev, drift_next)
-    finish(2, drift_prev, drift_next)
-
-    for m in packs + count_all + planes0 + count_g + late_packs + planes1:
+    move(LAST_LOW)
+    move(LAST_HIGH)
+    for m in moves[LAST_LOW] + moves[LAST_HIGH]:
+        m.start()
+    for part in (EDGE_HIGH, NEXT, LAST_LOW, LAST_HIGH):
+        finish(part, drift_prev, drift_next)
+
+    for m in packs + count_x + count_z + planes0 + count_g + late_packs + planes1:
         m.wait_send()
-    for pair in moves:
-        for m in pair:
+    for part in PARTS:
+        for m in moves[part]:
             m.wait_send()
 
 
-N_MESSAGES = (N_CURVE - 1) + 2 + 2 + 2 + 6 + 6 + 6
+N_MESSAGES = (NX - 1) + (NZ - 1) + 2 + 2 + 2 + 6 + 6 + 2 * len(PARTS)
 
 
 def local(state, coef, counts):
@@ -404,7 +427,7 @@
             vmem((8, 8, 2, 8, 128), f32), vmem((8, 8, 2, 8, 128), f32),
             vmem((8, 8, 2, 8, 128), f32), vmem((8, 8, 2, 8, 128), f32),
             vmem((8, 8, 17, 8, 128), f32),
-            vmem((N_CURVE, 1, 128), i32), vmem((2, 8, 128), i32), vmem((1, 128), i32), vmem((8, 128), i32),
+            vmem((NX, 1, 128), i32), vmem((NZ, NX, 1, 128), i32), vmem((2, 8, 128), i32), vmem((1, 128), i32), vmem((8, 128), i32),
             pltpu.SemaphoreType.DMA((3, 8)),
             pltpu.SemaphoreType.DMA((N_MESSAGES,)), pltpu.SemaphoreType.DMA((N_MESSAGES,)),
         ],

time: 39.8 us -> 38.3 us (0.962)
  Pallas kernels: 37.7 us -> 36.2 us
    pallas_call x1, Pallas kernels: 37.7 us -> 36.2 us  [local(): pl.pallas_call(kernel, out_shape=vmem((8, 8, 64, 128), f32), in_specs=[pl...]
where the time goes in v2:
time: 38.3 us; the launch traced here: 38.2 us
  Pallas kernels  36.2 us (95%)
  local copies, waits for them, and re-layouts  1.32 us (3%)
  between operations  0.66 us (2%)
    pallas_call x1, Pallas kernels, local(): pl.pallas_call(kernel, out_shape=vmem((8, 8, 64, 128), f32), in_specs=[pl...  36.2 us
    unnamed x1, local copies, waits for them, and re-layouts  1.32 us

profile of v2, /device:TPU:18, one launch (start us, length us, event | category | flops | bytes accessed | tf_op | source)
XLA Modules:
  0.0 38.2 jit_solution(9416433228440893575)
XLA Ops:
  0.7 36.2 %shard_map.37 = f32[8,8,64,128]{3,2,1,0:T(8,128)S(1)} custom-call(s32[1,1]{1,0:T(1,128)S(6)} %copy.7.counts, f32[2,8,8,96,128]{4,3,2,1,0:T(8,128)} %bitcast.4, f32[8,8,96,128]{3,2,1,0:T(8,128)} %bitcast.5), custom_call_target="tpu_custom_call" | custom-call | tf_op jit(solution)/shard_map/pallas_call | solution.py:410
  36.9 1.3 %copy.6 = f32[512,1,1024]{2,1,0:T(1,128)} copy(f32[512,1,1024]{2,1,0:T(1,128)S(1)} %bitcast.3) | data formatting | bytes 4194304

commit v3 on v2

--- a/solution.py
+++ b/solution.py
@@ -14,8 +14,8 @@
 CH = CAP // 128
 MESH = pl.DeviceIdType.MESH
 ORDER = (2, 3, 4, 5, 1, 6, 0, 7)
-INNER, EDGE_LOW, EDGE_HIGH, NEXT, LAST_LOW, LAST_HIGH = PARTS = (
-    (0, 4, 2, 4), (0, 4, 0, 2), (0, 4, 6, 2), (4, 2, 0, 8), (6, 1, 0, 8), (7, 1, 0, 8),
+INNER, MIDDLE, EDGE_LOW, EDGE_HIGH, NEXT, LAST_LOW, LAST_HIGH = PARTS = (
+    (0, 4, 2, 2), (0, 4, 4, 2), (0, 4, 0, 2), (0, 4, 6, 2), (4, 2, 0, 8), (6, 1, 0, 8), (7, 1, 0, 8),
 )
 
 
@@ -35,7 +35,7 @@
 
 def kernel(
     counts, state, coef, out,
-    raw_u, raw_s, raw_c, u0, u1, inv, yh, rx0, rx1, ts0, ts1, ps, pr, ls, lr,
+    raw_u, raw_s, raw_c, u0, u1, inv, yh, rx0_low, rx0_high, rx1_low, rx1_high, ts0, ts1, ps, pr, ls, lr,
     t2s, t2r, h2s, h2r, wide, cbx, cbz, cb3, cs, cs3,
 
     in_sem, send_sem, recv_sem,
@@ -68,6 +68,7 @@
     zero = jnp.zeros((8, 128), jnp.float32)
     held = counts[0, 0]
 
+    rx0, rx1 = (rx0_low, rx0_high), (rx1_low, rx1_high)
     index = [0]
 
     def message(src, dst, device, sends, receives):
@@ -110,21 +111,21 @@
             (0, 0, low, has_low, has_high), (1, 7, high, has_high, has_low),
         ):
             tails.append(message(
-                lambda d=d: ts.at[d], lambda d=d: rx.at[1 - d, :, pl.ds(0, 4)], (right, other),
+                lambda d=d: ts.at[d], lambda d=d: rx[1 - d].at[:, pl.ds(0, 4)], (right, other),
                 jnp.logical_and(sends, has_right), jnp.logical_and(receives, has_left)))
             heads.append(message(
                 lambda y=y: u.at[pl.ds(1, 8), y, pl.ds(0, 4)],
-                lambda d=d: rx.at[1 - d, :, pl.ds(16, 4)], (left, other),
+                lambda d=d: rx[1 - d].at[:, pl.ds(16, 4)], (left, other),
                 jnp.logical_and(sends, has_left), jnp.logical_and(receives, has_right)))
             mids.append(message(
-                lambda y=y: u.at[pl.ds(1, 8), y], lambda d=d: rx.at[1 - d, :, pl.ds(4, 12)],
+                lambda y=y: u.at[pl.ds(1, 8), y], lambda d=d: rx[1 - d].at[:, pl.ds(4, 12)],
                 (rank, other), sends, receives))
         return [tails[0], heads[0]], mids, [tails[1], heads[1]]
 
     planes0_low, planes0_mid, planes0_high = planes_out(u0, ts0, rx0)
     planes0 = planes0_low + planes0_mid + planes0_high
     planes1_low, planes1_mid, planes1_high = planes_out(u1, ts1, rx1)
-    planes1 = planes1_low + planes1_high + planes1_mid
+    planes1 = planes1_low + planes1_mid[:1] + planes1_high + planes1_mid[1:]
     moves = {}
     for part in PARTS:
         at = (pl.ds(part[0], part[1]), pl.ds(part[2], part[3]))
@@ -243,17 +244,18 @@
 
         loop(x_start, x_start + x_size, body, x_size)
 
-    def halos(rx, drift_prev):
-        starts = []
-        for side in range(2):
+    def halos(rx, drift_prev, sides=(0, 1)):
+        starts = {}
+        for side in sides:
             tile = cb3[side]
             other_prev = tile[0, 0] - rank * AVG
             other_next = tile[1, 0] - (rank + 1) * AVG
-            starts.append((AVG // 2 + drift_prev - other_prev, AVG + drift_prev - other_next))
+            starts[side] = (AVG // 2 + drift_prev - other_prev, AVG + drift_prev - other_next)
 
         def body(x):
-            for side, exists in ((0, has_low), (1, has_high)):
-                load = lambda k: rx[side, x, k]
+            for side in sides:
+                exists = (has_low, has_high)[side]
+                load = lambda k: rx[side][x, k]
                 begin, begin_next = starts[side]
                 own = shifted(load, begin, range(CH), 0, 8)
                 later = shifted(load, begin_next, range(4, CH), 4, 12)
@@ -263,7 +265,7 @@
                         value = jnp.where(lane + 128 * c >= 2 * AVG - begin_next, later[c], value)
                     yh[side, x, c] = jnp.where(exists, value, zero)
 
-        loop(0, 8, body, 4)
+        loop(0, 8, body, 8 // len(sides))
 
     def finish(part, drift_prev, drift_next):
         for m in moves[part]:
@@ -287,10 +289,12 @@
 
         loop(x_start, x_start + x_size, body, min(x_size, 8 // size))
 
-    for key in first_loads[:8]:
+    for key in first_loads[:4]:
         loads[key].wait()
     for key in other_loads:
         loads[key].start()
+    for key in first_loads[4:8]:
+        loads[key].wait()
     loop(0, 8, convert)
     cs[...] = jnp.full((1, 128), held, jnp.int32)
     cbx[xc] = jnp.full((1, 128), held, jnp.int32)
@@ -314,7 +318,7 @@
         ps[1, k] = lanes_packed(last_tile, last_lane, every)
 
     pl.semaphore_wait(barrier, len(peers))
-    for m in packs + count_x + planes0_low + planes0_mid:
+    for m in count_x + packs + planes0_low + planes0_mid:
         m.start()
 
     for key in other_loads:
@@ -322,9 +326,12 @@
     sweep(u0, True, range(1, 7), store_u1, (1, 7, 1))
     sweep(u1, False, range(2, 6), store_wide, (2, 6, 1))
     move(INNER)
+    for m in moves[INNER]:
+        m.start()
+    move(MIDDLE)
     for m in count_x:
         m.wait_recv()
-    for m in count_z + planes0_high + moves[INNER]:
+    for m in count_z + planes0_high + moves[MIDDLE]:
         m.start()
     for m in packs:
         m.wait_recv()
@@ -349,6 +356,8 @@
         m.start()
     sweep(u1, False, range(2, 6), store_wide, (6, 8, 1))
     move(EDGE_HIGH)
+    for m in moves[EDGE_HIGH]:
+        m.start()
 
     for m in count_z:
         m.wait_recv()
@@ -370,28 +379,34 @@
     plane_tails(u1, ts1)
     ls[0] = first_of(u1, 0, (0, 7))
     ls[1] = last_of(u1, 7, (0, 7))
-    for m in late_packs + planes1 + moves[EDGE_HIGH]:
+    for m in late_packs + planes1:
         m.start()
 
     sweep(u1, False, (1, 6), store_wide)
     move(NEXT)
     for m in moves[NEXT]:
         m.start()
-    finish(INNER, drift_prev, drift_next)
-    finish(EDGE_LOW, drift_prev, drift_next)
+    for part in (INNER, MIDDLE, EDGE_LOW, EDGE_HIGH):
+        finish(part, drift_prev, drift_next)
 
     for m in late_packs:
         m.wait_recv()
     fill_x(u1, jnp.where(has_left, lr[0], zero), jnp.where(has_right, lr[1], zero), (0, 7))
-    for m in planes1:
-        m.wait_recv()
-    halos(rx1, drift_prev)
-    sweep(u1, False, (0, 7), store_wide)
+    for m in planes1[:3]:
+        m.wait_recv()
+    halos(rx1, drift_prev, (1,))
+    sweep(u1, False, (7,), store_wide, (0, 8, 2))
+    move(LAST_HIGH)
+    for m in moves[LAST_HIGH]:
+        m.start()
+    for m in planes1[3:]:
+        m.wait_recv()
+    halos(rx1, drift_prev, (0,))
+    sweep(u1, False, (0,), store_wide, (0, 8, 2))
     move(LAST_LOW)
-    move(LAST_HIGH)
-    for m in moves[LAST_LOW] + moves[LAST_HIGH]:
-        m.start()
-    for part in (EDGE_HIGH, NEXT, LAST_LOW, LAST_HIGH):
+    for m in moves[LAST_LOW]:
+        m.start()
+    for part in (NEXT, LAST_HIGH, LAST_LOW):
         finish(part, drift_prev, drift_next)
 
     for m in packs + count_x + count_z + planes0 + count_g + late_packs + planes1:
@@ -420,7 +435,7 @@
             vmem((8, 8, 96, 128), f32), vmem((8, 8, 96, 128), f32), vmem((8, 8, 96, 128), f32),
             vmem((10, 8, CH, 8, 128), f32), vmem((10, 8, CH, 8, 128), f32), vmem((8, 8, CH, 8, 128), f32),
             vmem((2, 8, CH, 8, 128), f32),
-            vmem((2, 8, 25, 8, 128), f32), vmem((2, 8, 25, 8, 128), f32),
+            vmem((8, 25, 8, 128), f32), vmem((8, 25, 8, 128), f32), vmem((8, 25, 8, 128), f32), vmem((8, 25, 8, 128), f32),
             vmem((2, 8, 4, 8, 128), f32), vmem((2, 8, 4, 8, 128), f32),
             vmem((2, 4, 8, 128), f32), vmem((2, 4, 8, 128), f32),
             vmem((2, 8, 128), f32), vmem((2, 8, 128), f32),

time: 38.3 us -> 37.7 us (0.984); the launches traced: 38.2 us -> 37 us
  Pallas kernels: 36.2 us -> 35 us
    pallas_call x1, Pallas kernels: 36.2 us -> 35 us  [local(): pl.pallas_call(kernel, out_shape=vmem((8, 8, 64, 128), f32), in_specs=[pl...]
where the time goes in v3:
time: 37.7 us; the launch traced here: 37 us
  Pallas kernels  35 us (93%)
  local copies, waits for them, and re-layouts  1.32 us (4%)
  between operations  0.66 us (2%)
    pallas_call x1, Pallas kernels, local(): pl.pallas_call(kernel, out_shape=vmem((8, 8, 64, 128), f32), in_specs=[pl...  35 us
    unnamed x1, local copies, waits for them, and re-layouts  1.32 us

profile of v3, /device:TPU:18, one launch (start us, length us, event | category | flops | bytes accessed | tf_op | source)
XLA Modules:
  0.0 37.0 jit_solution(11584560195683622753)
XLA Ops:
  0.7 35.0 %shard_map.37 = f32[8,8,64,128]{3,2,1,0:T(8,128)S(1)} custom-call(s32[1,1]{1,0:T(1,128)S(6)} %copy.7.counts, f32[2,8,8,96,128]{4,3,2,1,0:T(8,128)} %bitcast.4, f32[8,8,96,128]{3,2,1,0:T(8,128)} %bitcast.5), custom_call_target="tpu_custom_call" | custom-call | tf_op jit(solution)/shard_map/pallas_call | solution.py:425
  35.7 1.3 %copy.6 = f32[512,1,1024]{2,1,0:T(1,128)} copy(f32[512,1,1024]{2,1,0:T(1,128)S(1)} %bitcast.3) | data formatting | bytes 4194304

commit v4 on v3

--- a/solution.py
+++ b/solution.py
@@ -14,8 +14,9 @@
 CH = CAP // 128
 MESH = pl.DeviceIdType.MESH
 ORDER = (2, 3, 4, 5, 1, 6, 0, 7)
-INNER, MIDDLE, EDGE_LOW, EDGE_HIGH, NEXT, LAST_LOW, LAST_HIGH = PARTS = (
-    (0, 4, 2, 2), (0, 4, 4, 2), (0, 4, 0, 2), (0, 4, 6, 2), (4, 2, 0, 8), (6, 1, 0, 8), (7, 1, 0, 8),
+INNER, MIDDLE, EDGE_LOW, EDGE_HIGH, NEXT, LOW_A, LOW_B, HIGH_A, HIGH_B = PARTS = (
+    (0, 4, 2, 2), (0, 4, 4, 2), (0, 4, 0, 2), (0, 4, 6, 2), (4, 2, 0, 8),
+    (6, 1, 0, 4), (6, 1, 4, 4), (7, 1, 0, 4), (7, 1, 4, 4),
 )
 
 
@@ -320,7 +321,6 @@
     pl.semaphore_wait(barrier, len(peers))
     for m in count_x + packs + planes0_low + planes0_mid:
         m.start()
-
     for key in other_loads:
         loads[key].wait()
     sweep(u0, True, range(1, 7), store_u1, (1, 7, 1))
@@ -395,18 +395,20 @@
     for m in planes1[:3]:
         m.wait_recv()
     halos(rx1, drift_prev, (1,))
-    sweep(u1, False, (7,), store_wide, (0, 8, 2))
-    move(LAST_HIGH)
-    for m in moves[LAST_HIGH]:
-        m.start()
+    for part in (HIGH_A, HIGH_B):
+        sweep(u1, False, (7,), store_wide, (part[2], part[2] + 4, 2))
+        move(part)
+        for m in moves[part]:
+            m.start()
     for m in planes1[3:]:
         m.wait_recv()
     halos(rx1, drift_prev, (0,))
-    sweep(u1, False, (0,), store_wide, (0, 8, 2))
-    move(LAST_LOW)
-    for m in moves[LAST_LOW]:
-        m.start()
-    for part in (NEXT, LAST_HIGH, LAST_LOW):
+    for part in (LOW_A, LOW_B):
+        sweep(u1, False, (0,), store_wide, (part[2], part[2] + 4, 2))
+        move(part)
+        for m in moves[part]:
+            m.start()
+    for part in (NEXT, HIGH_A, HIGH_B, LOW_A, LOW_B):
         finish(part, drift_prev, drift_next)
 
     for m in packs + count_x + count_z + planes0 + count_g + late_packs + planes1:

time: 37.7 us -> 37.6 us (level)
  no operation moved by 1% of the time
where the time goes in v4:
time: 37.6 us; the launch traced here: 37 us
  Pallas kernels  35 us (93%)
  local copies, waits for them, and re-layouts  1.32 us (4%)
  between operations  0.66 us (2%)
    pallas_call x1, Pallas kernels, local(): pl.pallas_call(kernel, out_shape=vmem((8, 8, 64, 128), f32), in_specs=[pl...  35 us
    unnamed x1, local copies, waits for them, and re-layouts  1.32 us

profile of v4, /device:TPU:18, one launch (start us, length us, event | category | flops | bytes accessed | tf_op | source)
XLA Modules:
  0.0 37.0 jit_solution(9152128295740017523)
XLA Ops:
  0.7 35.0 %shard_map.37 = f32[8,8,64,128]{3,2,1,0:T(8,128)S(1)} custom-call(s32[1,1]{1,0:T(1,128)S(6)} %copy.7.counts, f32[2,8,8,96,128]{4,3,2,1,0:T(8,128)} %bitcast.4, f32[8,8,96,128]{3,2,1,0:T(8,128)} %bitcast.5), custom_call_target="tpu_custom_call" | custom-call | tf_op jit(solution)/shard_map/pallas_call | solution.py:427
  35.6 1.3 %copy.6 = f32[512,1,1024]{2,1,0:T(1,128)} copy(f32[512,1,1024]{2,1,0:T(1,128)S(1)} %bitcast.3) | data formatting | bytes 4194304
